TPU v7x, 32 devices: a whole 2x2x4 slice. The times are simulated.
32 devices in a mesh: row: 8 (over y, x, core), col: 4 (over z).
Axes of the slice: x: 2, y: 2, z: 4, core: 2. Of those that a mesh axis runs over, the one named last changes fastest.
Arguments:
- singular_vectors: float32 [4096, 4096], P('row', 'col'), may hold values from -6 to 6
- reflector_vectors: float32 [2, 16, 256, 512], P(None, 'row', 'col'), may hold values from -2 to 2, as said below
- reflector_factors: float32 [2, 16, 256, 256], P(None, 'row', 'col'), as said below
- sweep_bounds: int32 [2, 2], replicated, may hold values from 0 to 3584, as said below
Outputs:
- transformed: float32 [4096, 4096], P('row', 'col')
Inputs may be any that keep to these rules, and one draw needn't show every extreme that they name: `reflector_vectors`: row j of each block's 256 x 2 * 256 slice is a reflector: 1 at position j, nonzero only at positions j to j + 255. `reflector_factors`: each block's factor is the upper triangular inverse of the strictly upper part of W W^T plus half of its diagonal, W being that block's slice of reflector_vectors, so that each block's transformation is orthogonal. `sweep_bounds`: both entries are multiples of 256, and the first is below the second.
All inputs are finite; a program needn't handle non-finite values.
Results may differ from a plain program's by a relative error of at most 0.0003.
Values sent between devices are 32-bit elements; how exact they have to be, the bound alone decides.
A program may use at most 64 MiB of HBM per device.

v0:
```python
import jax
import jax.numpy as jnp
from jax import lax
from jax.sharding import PartitionSpec as P

exact_mode = lax.Precision.HIGHEST


def extended_2(block, sides, width):
    for axis, dim in sides:
        count = lax.axis_size(axis)
        forward = [(i, i + 1) for i in range(count - 1)]
        backward = [(target, source) for source, target in forward]
        low = lax.ppermute(
            lax.slice_in_dim(block, block.shape[dim] - width, None, axis=dim), axis, forward
        )
        high = lax.ppermute(lax.slice_in_dim(block, 0, width, axis=dim), axis, backward)
        block = jnp.concatenate([low, block, high], axis=dim)
    return block


def apply_block(row_block, vectors, factor):
    inner_part = jnp.dot(
        vectors, row_block, precision=exact_mode, preferred_element_type=jnp.float32
    )
    inner_part = jnp.dot(
        factor, inner_part, precision=exact_mode, preferred_element_type=jnp.float32
    )
    return row_block - jnp.dot(
        vectors.T, inner_part, precision=exact_mode, preferred_element_type=jnp.float32
    )


def keep_same(operand):
    return operand


def per_device(singular_vectors, reflector_vectors, reflector_factors, sweep_bounds):
    row_count = lax.axis_size("row")
    owner_row = lax.axis_index("row")
    row_dev, col_count = singular_vectors.shape
    reflect = reflector_vectors.shape[3] // 2
    blocks_dev = row_dev // reflect
    sweep_count = reflector_vectors.shape[0]
    vectors_all, factors_all = (
        lax.all_gather(reflector_vectors, "col", axis=2, tiled=True),
        lax.all_gather(reflector_factors, "col", axis=2, tiled=True),
    )
    pieces = 4
    piece_cols = col_count // pieces
    unit_count = sweep_count * pieces
    steps_total = row_count - 1 + unit_count
    lag_steps = row_count - 1 - owner_row

    def one_step(step_id, state_pair):
        field_now, below_rows = state_pair
        unit_now = step_id - lag_steps
        active = (unit_now >= 0) & (unit_now < unit_count)
        unit_safe = jnp.clip(unit_now, 0, unit_count - 1)
        col_start = unit_safe % pieces * piece_cols
        sweep_id = unit_safe // pieces
        first_row = sweep_bounds[sweep_id, 0]
        last_row = sweep_bounds[sweep_id, 1]
        vec_sweep = lax.dynamic_index_in_dim(vectors_all, sweep_id, 0, keepdims=False)
        fac_sweep = lax.dynamic_index_in_dim(factors_all, sweep_id, 0, keepdims=False)

        def work(operand):
            field_in, below_in = operand
            own_part = lax.dynamic_slice_in_dim(field_in, col_start, piece_cols, 1)
            extended = jnp.concatenate([own_part, below_in], axis=0)

            def one_block(counter, current):
                local_id = blocks_dev - 1 - counter
                start_row = (owner_row * blocks_dev + local_id) * reflect
                is_live = (start_row >= first_row) & (start_row <= last_row)

                def update(matrix):
                    row_block = lax.dynamic_slice_in_dim(matrix, local_id * reflect, 2 * reflect, 0)
                    vectors = lax.dynamic_index_in_dim(vec_sweep, local_id, 0, keepdims=False)
                    factor = lax.dynamic_index_in_dim(fac_sweep, local_id, 0, keepdims=False)
                    row_block = apply_block(row_block, vectors, factor)
                    return lax.dynamic_update_slice_in_dim(matrix, row_block, local_id * reflect, 0)

                return lax.cond(is_live, update, keep_same, current)

            extended = lax.fori_loop(0, blocks_dev, one_block, extended)
            field_out = lax.dynamic_update_slice_in_dim(field_in, extended[:row_dev], col_start, 1)
            return (field_out, extended[row_dev:])

        field_now, returned = lax.cond(active, work, keep_same, (field_now, below_rows))
        top_rows = lax.dynamic_slice(field_now, (0, col_start), (reflect, piece_cols))
        message = jnp.concatenate([top_rows, returned], axis=0)
        padded = extended_2(message, (("row", 0),), reflect)
        from_left = padded[:reflect]
        below_next = padded[3 * reflect :]
        prior = unit_now - 1
        valid = (owner_row > 0) & (prior >= 0) & (prior < unit_count)
        prior_col = jnp.clip(prior, 0, unit_count - 1) % pieces * piece_cols
        current_top = lax.dynamic_slice(field_now, (0, prior_col), (reflect, piece_cols))
        field_now = lax.dynamic_update_slice(
            field_now, jnp.where(valid, from_left, current_top), (0, prior_col)
        )
        return (field_now, below_next)

    def two_steps(pair_id, state_pair):
        return one_step(2 * pair_id + 1, one_step(2 * pair_id, state_pair))

    below_start = jnp.zeros((reflect, piece_cols), jnp.float32)
    pair_count = (steps_total + 1) // 2
    result_field, below_last = lax.fori_loop(
        0, pair_count, two_steps, (singular_vectors, below_start)
    )
    return result_field


def solution(mesh):
    placed = (P("row", "col"), P(None, "row", "col", None), P(None, "row", "col", None), P())
    return jax.shard_map(
        per_device, mesh=mesh, in_specs=placed, out_specs=P("row", "col"), check_vma=False
    )
```

profile of v0, /device:TPU:1, one launch (start us, length us, event | category | flops | bytes accessed | tf_op | source)
XLA Modules:
  0.0 527.2 jit_solution(4495330475815302078)
XLA Ops:
  6.5 3.2 copy.45
  10.5 29.0 %all-gather.5.cloned.1.call-done = f32[2,2,256,256]{3,2,1,0:T(8,128)} async-done(((f32[2,2,64,256]{3,2,1,0:T(8,128)}), f32[2,2,256,256]{3,2,1,0:T(8,128)}) %all-gather.5.cloned.1.call-update) | async-done | bytes 1048592 | tf_op jit(solution)/shard_map/all_gather | solution.py:47
  39.5 46.9 %all-gather.3.cloned.1.call-done = f32[2,2,256,512]{3,2,1,0:T(8,128)} async-done(((f32[2,2,64,512]{3,2,1,0:T(8,128)}), f32[2,2,256,512]{3,2,1,0:T(8,128)}) %all-gather.3.cloned.1.call-update) | async-done | bytes 2097168 | tf_op jit(solution)/shard_map/all_gather | solution.py:46
  86.4 433.9 %while.66 = (s32[]{:T(128)}, f32[512,1024]{1,0:T(8,128)}, f32[256,256]{1,0:T(8,128)S(1)}, s32[]{:T(128)}, s32[2,2]{1,0:T(2,128)S(1)}, /*index=5*/f32[2,2,256,512...) while((s32[]{:T(128)}, f32[512,1024]{1,0:T(8,128)}, ...), condition=%wide.region_13.14_spmd, body=%wide.region_0.13_spmd.sunk | while | flops 2014052352 | bytes 39848304 | solution.py:110
  86.5 3.8 collective-permute-start
  90.3 3.3 collective-permute-done
  97.3 6.5 %collective-permute-done.1 = f32[256,256]{1,0:T(8,128)S(1)} collective-permute-done((f32[256,256]{1,0:T(8,128)S(1)}, f32[256,256]{1,0:T(8,128)S(1)}, u32[]{:S(2)}, u32[]{:S(2)}) %collective-permute-start.1) | collective-permute-done | bytes 262176 | tf_op jit(solution)/shard_map/while/body/eval_jaxpr/ppermute | solution.py:17
  105.8 3.3 collective-permute-done.2
  112.8 6.5 %collective-permute-done.3 = f32[256,256]{1,0:T(8,128)S(1)} collective-permute-done((f32[256,256]{1,0:T(8,128)S(1)}, f32[256,256]{1,0:T(8,128)S(1)}, u32[]{:S(2)}, u32[]{:S(2)}) %collective-permute-start.3) | collective-permute-done | bytes 262176 | tf_op jit(solution)/shard_map/while/body/eval_jaxpr/ppermute | solution.py:17
  121.2 3.3 collective-permute-done
  128.2 6.9 %collective-permute-done.1 = f32[256,256]{1,0:T(8,128)S(1)} collective-permute-done((f32[256,256]{1,0:T(8,128)S(1)}, f32[256,256]{1,0:T(8,128)S(1)}, u32[]{:S(2)}, u32[]{:S(2)}) %collective-permute-start.1) | collective-permute-done | bytes 262176 | tf_op jit(solution)/shard_map/while/body/eval_jaxpr/ppermute | solution.py:17
  135.1 13.0 %collective-permute-start.2 = (f32[256,256]{1,0:T(8,128)S(1)}, f32[256,256]{1,0:T(8,128)S(1)}, u32[]{:S(2)}, u32[]{:S(2)}) collective-permute-start(f32[256,256]{1,0:T(8,128)S(1)} %get-tuple-element.1135), channel_id=1, source_target_pairs={{0,4},{4,8},{8,12},{12,16},{16,20},{20,24},{24,28},{1,5},{5,9},{9,... | collective-permute-start | bytes 786440 | tf_op jit(solution)/shard_map/while/body/eval_jaxpr/ppermute | solution.py:14
  148.2 3.3 collective-permute-done.2
  155.2 21.6 %collective-permute-done.3 = f32[256,256]{1,0:T(8,128)S(1)} collective-permute-done((f32[256,256]{1,0:T(8,128)S(1)}, f32[256,256]{1,0:T(8,128)S(1)}, u32[]{:S(2)}, u32[]{:S(2)}) %collective-permute-start.3) | collective-permute-done | bytes 262176 | tf_op jit(solution)/shard_map/while/body/eval_jaxpr/ppermute | solution.py:17
  176.7 14.2 %collective-permute-start = (f32[256,256]{1,0:T(8,128)S(1)}, f32[256,256]{1,0:T(8,128)S(1)}, u32[]{:S(2)}, u32[]{:S(2)}) collective-permute-start(f32[256,256]{1,0:T(8,128)S(1)} %get-tuple-element.1131), channel_id=1, source_target_pairs={{0,4},{4,8},{8,12},{12,16},{16,20},{20,24},{24,28},{1,5},{5,9},{9,... | collective-permute-start | bytes 786440 | tf_op jit(solution)/shard_map/while/body/eval_jaxpr/ppermute | solution.py:14
  190.9 3.3 collective-permute-done
  197.9 21.6 %collective-permute-done.1 = f32[256,256]{1,0:T(8,128)S(1)} collective-permute-done((f32[256,256]{1,0:T(8,128)S(1)}, f32[256,256]{1,0:T(8,128)S(1)}, u32[]{:S(2)}, u32[]{:S(2)}) %collective-permute-start.1) | collective-permute-done | bytes 262176 | tf_op jit(solution)/shard_map/while/body/eval_jaxpr/ppermute | solution.py:17
  219.5 15.1 %collective-permute-start.2 = (f32[256,256]{1,0:T(8,128)S(1)}, f32[256,256]{1,0:T(8,128)S(1)}, u32[]{:S(2)}, u32[]{:S(2)}) collective-permute-start(f32[256,256]{1,0:T(8,128)S(1)} %get-tuple-element.1135), channel_id=1, source_target_pairs={{0,4},{4,8},{8,12},{12,16},{16,20},{20,24},{24,28},{1,5},{5,9},{9,... | collective-permute-start | bytes 786440 | tf_op jit(solution)/shard_map/while/body/eval_jaxpr/ppermute | solution.py:14
  234.6 3.3 collective-permute-done.2
  241.6 7.6 %collective-permute-done.3 = f32[256,256]{1,0:T(8,128)S(1)} collective-permute-done((f32[256,256]{1,0:T(8,128)S(1)}, f32[256,256]{1,0:T(8,128)S(1)}, u32[]{:S(2)}, u32[]{:S(2)}) %collective-permute-start.3) | collective-permute-done | bytes 262176 | tf_op jit(solution)/shard_map/while/body/eval_jaxpr/ppermute | solution.py:17
  249.2 13.3 %conditional.8 = ((f32[512,1024]{1,0:T(8,128)}, f32[256,256]{1,0:T(8,128)S(1)})) conditional(s32[]{:T(128)} %convert_element_type.45, (f32[512,1024]{1,0:T(8,128)}, f32[256,256]{1,0:T(8,128)S(1)}) %tuple.171, (s32[]{:T(128)}, f32[512,1024]{1,0:T(8,128)}, f32[256,256]{1,0:T(8,128)S(1)}, s32[]{:T(128)}, pred[]{:T(512)}, ...), branch_computations={%region_1.1_spmd, %region_2.6_spmd} | conditional | flops 1006960640 | bytes 16515680 | solution.py:90
  252.5 6.4 %while.64 = (s32[]{:T(128)}, f32[768,256]{1,0:T(8,128)S(1)}, s32[]{:T(128)}, s32[]{:T(128)}, s32[]{:T(128)}, /*index=5*/f32[2,256,512]{2,1,0:T(8,128)S(1)}, f32[2,256,256]{2,1,0:T(8,128)S(1)}, s32[]{:T(128)}, s32[]{:T(128)}) while((s32[]{:T(128)}, f32[768,256]{1,0:T(8,128)S(1)}, s32[]{:T(128)}, s32[]{:T(128)}, s32[]{:T(128)}, ...), condition=%wide.region_6.5_spmd, body=%wide.region_3.4_spmd.sunk | while | flops 1006764032 | bytes 3932463 | solution.py:86
  259.0 3.5 dynamic_update_slice.35
  264.4 3.3 collective-permute-done
  271.4 7.4 %collective-permute-done.1 = f32[256,256]{1,0:T(8,128)S(1)} collective-permute-done((f32[256,256]{1,0:T(8,128)S(1)}, f32[256,256]{1,0:T(8,128)S(1)}, u32[]{:S(2)}, u32[]{:S(2)}) %collective-permute-start.1) | collective-permute-done | bytes 262176 | tf_op jit(solution)/shard_map/while/body/eval_jaxpr/ppermute | solution.py:17
  278.8 13.3 %conditional.9 = ((f32[512,1024]{1,0:T(8,128)}, f32[256,256]{1,0:T(8,128)S(1)})) conditional(s32[]{:T(128)} %convert_element_type.44, (f32[512,1024]{1,0:T(8,128)}, f32[256,256]{1,0:T(8,128)S(1)}) %tuple.173, (s32[]{:T(128)}, f32[512,1024]{1,0:T(8,128)}, f32[256,256]{1,0:T(8,128)S(1)}, s32[]{:T(128)}, pred[]{:T(512)}, ...), branch_computations={%region_7.7_spmd, %region_8.12_spmd} | conditional | flops 1006960640 | bytes 16515680 | solution.py:90
  282.1 6.4 %while.65 = (s32[]{:T(128)}, f32[768,256]{1,0:T(8,128)S(1)}, s32[]{:T(128)}, s32[]{:T(128)}, s32[]{:T(128)}, /*index=5*/f32[2,256,512]{2,1,0:T(8,128)S(1)}, f32[2,256,256]{2,1,0:T(8,128)S(1)}, s32[]{:T(128)}, s32[]{:T(128)}) while((s32[]{:T(128)}, f32[768,256]{1,0:T(8,128)S(1)}, s32[]{:T(128)}, s32[]{:T(128)}, s32[]{:T(128)}, ...), condition=%wide.region_12.11_spmd, body=%wide.region_9.10_spmd.sunk | while | flops 1006764032 | bytes 3932463 | solution.py:86
  288.6 3.5 dynamic_update_slice.37
  294.1 3.3 collective-permute-done.2
  301.0 6.7 %collective-permute-done.3 = f32[256,256]{1,0:T(8,128)S(1)} collective-permute-done((f32[256,256]{1,0:T(8,128)S(1)}, f32[256,256]{1,0:T(8,128)S(1)}, u32[]{:S(2)}, u32[]{:S(2)}) %collective-permute-start.3) | collective-permute-done | bytes 262176 | tf_op jit(solution)/shard_map/while/body/eval_jaxpr/ppermute | solution.py:17
  307.7 13.3 %conditional.8 = ((f32[512,1024]{1,0:T(8,128)}, f32[256,256]{1,0:T(8,128)S(1)})) conditional(s32[]{:T(128)} %convert_element_type.45, (f32[512,1024]{1,0:T(8,128)}, f32[256,256]{1,0:T(8,128)S(1)}) %tuple.171, (s32[]{:T(128)}, f32[512,1024]{1,0:T(8,128)}, f32[256,256]{1,0:T(8,128)S(1)}, s32[]{:T(128)}, pred[]{:T(512)}, ...), branch_computations={%region_1.1_spmd, %region_2.6_spmd} | conditional | flops 1006960640 | bytes 16515680 | solution.py:90
  311.1 6.4 %while.64 = (s32[]{:T(128)}, f32[768,256]{1,0:T(8,128)S(1)}, s32[]{:T(128)}, s32[]{:T(128)}, s32[]{:T(128)}, /*index=5*/f32[2,256,512]{2,1,0:T(8,128)S(1)}, f32[2,256,256]{2,1,0:T(8,128)S(1)}, s32[]{:T(128)}, s32[]{:T(128)}) while((s32[]{:T(128)}, f32[768,256]{1,0:T(8,128)S(1)}, s32[]{:T(128)}, s32[]{:T(128)}, s32[]{:T(128)}, ...), condition=%wide.region_6.5_spmd, body=%wide.region_3.4_spmd.sunk | while | flops 1006764032 | bytes 3932463 | solution.py:86
  317.6 3.5 dynamic_update_slice.35
  323.0 3.3 collective-permute-done
  330.0 7.9 %collective-permute-done.1 = f32[256,256]{1,0:T(8,128)S(1)} collective-permute-done((f32[256,256]{1,0:T(8,128)S(1)}, f32[256,256]{1,0:T(8,128)S(1)}, u32[]{:S(2)}, u32[]{:S(2)}) %collective-permute-start.1) | collective-permute-done | bytes 262176 | tf_op jit(solution)/shard_map/while/body/eval_jaxpr/ppermute | solution.py:17
  337.9 12.6 %conditional.9 = ((f32[512,1024]{1,0:T(8,128)}, f32[256,256]{1,0:T(8,128)S(1)})) conditional(s32[]{:T(128)} %convert_element_type.44, (f32[512,1024]{1,0:T(8,128)}, f32[256,256]{1,0:T(8,128)S(1)}) %tuple.173, (s32[]{:T(128)}, f32[512,1024]{1,0:T(8,128)}, f32[256,256]{1,0:T(8,128)S(1)}, s32[]{:T(128)}, pred[]{:T(512)}, ...), branch_computations={%region_7.7_spmd, %region_8.12_spmd} | conditional | flops 1006960640 | bytes 16515680 | solution.py:90
  341.2 6.4 %while.65 = (s32[]{:T(128)}, f32[768,256]{1,0:T(8,128)S(1)}, s32[]{:T(128)}, s32[]{:T(128)}, s32[]{:T(128)}, /*index=5*/f32[2,256,512]{2,1,0:T(8,128)S(1)}, f32[2,256,256]{2,1,0:T(8,128)S(1)}, s32[]{:T(128)}, s32[]{:T(128)}) while((s32[]{:T(128)}, f32[768,256]{1,0:T(8,128)S(1)}, s32[]{:T(128)}, s32[]{:T(128)}, s32[]{:T(128)}, ...), condition=%wide.region_12.11_spmd, body=%wide.region_9.10_spmd.sunk | while | flops 1006764032 | bytes 3932463 | solution.py:86
  347.6 2.9 dynamic_update_slice.37
  353.0 3.3 collective-permute-done.2
  360.0 7.6 %collective-permute-done.3 = f32[256,256]{1,0:T(8,128)S(1)} collective-permute-done((f32[256,256]{1,0:T(8,128)S(1)}, f32[256,256]{1,0:T(8,128)S(1)}, u32[]{:S(2)}, u32[]{:S(2)}) %collective-permute-start.3) | collective-permute-done | bytes 262176 | tf_op jit(solution)/shard_map/while/body/eval_jaxpr/ppermute | solution.py:17
  367.5 13.3 %conditional.8 = ((f32[512,1024]{1,0:T(8,128)}, f32[256,256]{1,0:T(8,128)S(1)})) conditional(s32[]{:T(128)} %convert_element_type.45, (f32[512,1024]{1,0:T(8,128)}, f32[256,256]{1,0:T(8,128)S(1)}) %tuple.171, (s32[]{:T(128)}, f32[512,1024]{1,0:T(8,128)}, f32[256,256]{1,0:T(8,128)S(1)}, s32[]{:T(128)}, pred[]{:T(512)}, ...), branch_computations={%region_1.1_spmd, %region_2.6_spmd} | conditional | flops 1006960640 | bytes 16515680 | solution.py:90
  370.9 6.4 %while.64 = (s32[]{:T(128)}, f32[768,256]{1,0:T(8,128)S(1)}, s32[]{:T(128)}, s32[]{:T(128)}, s32[]{:T(128)}, /*index=5*/f32[2,256,512]{2,1,0:T(8,128)S(1)}, f32[2,256,256]{2,1,0:T(8,128)S(1)}, s32[]{:T(128)}, s32[]{:T(128)}) while((s32[]{:T(128)}, f32[768,256]{1,0:T(8,128)S(1)}, s32[]{:T(128)}, s32[]{:T(128)}, s32[]{:T(128)}, ...), condition=%wide.region_6.5_spmd, body=%wide.region_3.4_spmd.sunk | while | flops 1006764032 | bytes 3932463 | solution.py:86
  377.4 3.5 dynamic_update_slice.35
  382.8 3.3 collective-permute-done
  389.8 7.4 %collective-permute-done.1 = f32[256,256]{1,0:T(8,128)S(1)} collective-permute-done((f32[256,256]{1,0:T(8,128)S(1)}, f32[256,256]{1,0:T(8,128)S(1)}, u32[]{:S(2)}, u32[]{:S(2)}) %collective-permute-start.1) | collective-permute-done | bytes 262176 | tf_op jit(solution)/shard_map/while/body/eval_jaxpr/ppermute | solution.py:17
  397.2 13.3 %conditional.9 = ((f32[512,1024]{1,0:T(8,128)}, f32[256,256]{1,0:T(8,128)S(1)})) conditional(s32[]{:T(128)} %convert_element_type.44, (f32[512,1024]{1,0:T(8,128)}, f32[256,256]{1,0:T(8,128)S(1)}) %tuple.173, (s32[]{:T(128)}, f32[512,1024]{1,0:T(8,128)}, f32[256,256]{1,0:T(8,128)S(1)}, s32[]{:T(128)}, pred[]{:T(512)}, ...), branch_computations={%region_7.7_spmd, %region_8.12_spmd} | conditional | flops 1006960640 | bytes 16515680 | solution.py:90
  400.5 6.4 %while.65 = (s32[]{:T(128)}, f32[768,256]{1,0:T(8,128)S(1)}, s32[]{:T(128)}, s32[]{:T(128)}, s32[]{:T(128)}, /*index=5*/f32[2,256,512]{2,1,0:T(8,128)S(1)}, f32[2,256,256]{2,1,0:T(8,128)S(1)}, s32[]{:T(128)}, s32[]{:T(128)}) while((s32[]{:T(128)}, f32[768,256]{1,0:T(8,128)S(1)}, s32[]{:T(128)}, s32[]{:T(128)}, s32[]{:T(128)}, ...), condition=%wide.region_12.11_spmd, body=%wide.region_9.10_spmd.sunk | while | flops 1006764032 | bytes 3932463 | solution.py:86
  407.0 3.5 dynamic_update_slice.37
  412.4 3.3 collective-permute-done.2
  419.4 6.7 %collective-permute-done.3 = f32[256,256]{1,0:T(8,128)S(1)} collective-permute-done((f32[256,256]{1,0:T(8,128)S(1)}, f32[256,256]{1,0:T(8,128)S(1)}, u32[]{:S(2)}, u32[]{:S(2)}) %collective-permute-start.3) | collective-permute-done | bytes 262176 | tf_op jit(solution)/shard_map/while/body/eval_jaxpr/ppermute | solution.py:17
  426.1 13.3 %conditional.8 = ((f32[512,1024]{1,0:T(8,128)}, f32[256,256]{1,0:T(8,128)S(1)})) conditional(s32[]{:T(128)} %convert_element_type.45, (f32[512,1024]{1,0:T(8,128)}, f32[256,256]{1,0:T(8,128)S(1)}) %tuple.171, (s32[]{:T(128)}, f32[512,1024]{1,0:T(8,128)}, f32[256,256]{1,0:T(8,128)S(1)}, s32[]{:T(128)}, pred[]{:T(512)}, ...), branch_computations={%region_1.1_spmd, %region_2.6_spmd} | conditional | flops 1006960640 | bytes 16515680 | solution.py:90
  429.5 6.4 %while.64 = (s32[]{:T(128)}, f32[768,256]{1,0:T(8,128)S(1)}, s32[]{:T(128)}, s32[]{:T(128)}, s32[]{:T(128)}, /*index=5*/f32[2,256,512]{2,1,0:T(8,128)S(1)}, f32[2,256,256]{2,1,0:T(8,128)S(1)}, s32[]{:T(128)}, s32[]{:T(128)}) while((s32[]{:T(128)}, f32[768,256]{1,0:T(8,128)S(1)}, s32[]{:T(128)}, s32[]{:T(128)}, s32[]{:T(128)}, ...), condition=%wide.region_6.5_spmd, body=%wide.region_3.4_spmd.sunk | while | flops 1006764032 | bytes 3932463 | solution.py:86
  435.9 3.5 dynamic_update_slice.35
  441.4 3.3 collective-permute-done
  448.4 6.5 %collective-permute-done.1 = f32[256,256]{1,0:T(8,128)S(1)} collective-permute-done((f32[256,256]{1,0:T(8,128)S(1)}, f32[256,256]{1,0:T(8,128)S(1)}, u32[]{:S(2)}, u32[]{:S(2)}) %collective-permute-start.1) | collective-permute-done | bytes 262176 | tf_op jit(solution)/shard_map/while/body/eval_jaxpr/ppermute | solution.py:17
  454.9 12.6 %conditional.9 = ((f32[512,1024]{1,0:T(8,128)}, f32[256,256]{1,0:T(8,128)S(1)})) conditional(s32[]{:T(128)} %convert_element_type.44, (f32[512,1024]{1,0:T(8,128)}, f32[256,256]{1,0:T(8,128)S(1)}) %tuple.173, (s32[]{:T(128)}, f32[512,1024]{1,0:T(8,128)}, f32[256,256]{1,0:T(8,128)S(1)}, s32[]{:T(128)}, pred[]{:T(512)}, ...), branch_computations={%region_7.7_spmd, %region_8.12_spmd} | conditional | flops 1006960640 | bytes 16515680 | solution.py:90
  458.1 6.4 %while.65 = (s32[]{:T(128)}, f32[768,256]{1,0:T(8,128)S(1)}, s32[]{:T(128)}, s32[]{:T(128)}, s32[]{:T(128)}, /*index=5*/f32[2,256,512]{2,1,0:T(8,128)S(1)}, f32[2,256,256]{2,1,0:T(8,128)S(1)}, s32[]{:T(128)}, s32[]{:T(128)}) while((s32[]{:T(128)}, f32[768,256]{1,0:T(8,128)S(1)}, s32[]{:T(128)}, s32[]{:T(128)}, s32[]{:T(128)}, ...), condition=%wide.region_12.11_spmd, body=%wide.region_9.10_spmd.sunk | while | flops 1006764032 | bytes 3932463 | solution.py:86
  464.6 2.9 dynamic_update_slice.37
  469.4 3.3 collective-permute-done.2
  476.4 6.5 %collective-permute-done.3 = f32[256,256]{1,0:T(8,128)S(1)} collective-permute-done((f32[256,256]{1,0:T(8,128)S(1)}, f32[256,256]{1,0:T(8,128)S(1)}, u32[]{:S(2)}, u32[]{:S(2)}) %collective-permute-start.3) | collective-permute-done | bytes 262176 | tf_op jit(solution)/shard_map/while/body/eval_jaxpr/ppermute | solution.py:17
  484.9 8.0 %collective-permute-done = f32[256,256]{1,0:T(8,128)S(1)} collective-permute-done((f32[256,256]{1,0:T(8,128)S(1)}, f32[256,256]{1,0:T(8,128)S(1)}, u32[]{:S(2)}, u32[]{:S(2)}) %collective-permute-start) | collective-permute-done | bytes 262176 | tf_op jit(solution)/shard_map/while/body/eval_jaxpr/ppermute | solution.py:14
  496.7 8.2 %collective-permute-done.1 = f32[256,256]{1,0:T(8,128)S(1)} collective-permute-done((f32[256,256]{1,0:T(8,128)S(1)}, f32[256,256]{1,0:T(8,128)S(1)}, u32[]{:S(2)}, u32[]{:S(2)}) %collective-permute-start.1) | collective-permute-done | bytes 262176 | tf_op jit(solution)/shard_map/while/body/eval_jaxpr/ppermute | solution.py:17
  506.8 3.3 collective-permute-done.2
  513.8 6.5 %collective-permute-done.3 = f32[256,256]{1,0:T(8,128)S(1)} collective-permute-done((f32[256,256]{1,0:T(8,128)S(1)}, f32[256,256]{1,0:T(8,128)S(1)}, u32[]{:S(2)}, u32[]{:S(2)}) %collective-permute-start.3) | collective-permute-done | bytes 262176 | tf_op jit(solution)/shard_map/while/body/eval_jaxpr/ppermute | solution.py:17
  (195 shorter events, 175.3 us)
Async XLA Ops:
  6.5 79.9 %copy-start.2 = (s32[2,2]{1,0:T(2,128)S(1)}, s32[2,2]{1,0:T(2,128)}, u32[]{:S(2)}) copy-start(s32[2,2]{1,0:T(2,128)} %param.21) | copy-start | bytes 52
  6.5 32.9 %all-gather.5.cloned.1.call-start = ((), (), s32[]{:S(2)}) async-start(), calls=%async_computation.1 | async-start | bytes 1310720 | tf_op jit(solution)/shard_map/all_gather | solution.py:47
  9.7 76.7 %all-gather.3.cloned.1.call-start = ((), (), s32[]{:S(2)}) async-start(), calls=%async_computation | async-start | bytes 2621440 | tf_op jit(solution)/shard_map/all_gather | solution.py:46
  86.5 7.1 %collective-permute-start = (f32[256,256]{1,0:T(8,128)S(1)}, f32[256,256]{1,0:T(8,128)S(1)}, u32[]{:S(2)}, u32[]{:S(2)}) collective-permute-start(f32[256,256]{1,0:T(8,128)S(1)} %get-tuple-element.1131), channel_id=1, source_target_pairs={{0,4},{4,8},{8,12},{12,16},{16,20},{20,24},{24,28},{1,5},{5,9},{9,... | collective-permute-start | bytes 786440 | tf_op jit(solution)/shard_map/while/body/eval_jaxpr/ppermute | solution.py:14
  95.4 8.4 %collective-permute-start.1 = (f32[256,256]{1,0:T(8,128)S(1)}, f32[256,256]{1,0:T(8,128)S(1)}, u32[]{:S(2)}, u32[]{:S(2)}) collective-permute-start(f32[256,256]{1,0:T(8,128)S(1)} %get-tuple-element.1133), channel_id=1, source_target_pairs={{4,0},{8,4},{12,8},{16,12},{20,16},{24,20},{28,24},{5,1},{9,5},{13... | collective-permute-start | bytes 786440 | tf_op jit(solution)/shard_map/while/body/eval_jaxpr/ppermute | solution.py:17
  103.8 5.2 collective-permute-start.2
  110.8 8.4 %collective-permute-start.3 = (f32[256,256]{1,0:T(8,128)S(1)}, f32[256,256]{1,0:T(8,128)S(1)}, u32[]{:S(2)}, u32[]{:S(2)}) collective-permute-start(f32[256,256]{1,0:T(8,128)S(1)} %get-tuple-element.1137), channel_id=1, source_target_pairs={{4,0},{8,4},{12,8},{16,12},{20,16},{24,20},{28,24},{5,1},{9,5},{13... | collective-permute-start | bytes 786440 | tf_op jit(solution)/shard_map/while/body/eval_jaxpr/ppermute | solution.py:17
  119.3 5.2 collective-permute-start
  126.3 8.9 %collective-permute-start.1 = (f32[256,256]{1,0:T(8,128)S(1)}, f32[256,256]{1,0:T(8,128)S(1)}, u32[]{:S(2)}, u32[]{:S(2)}) collective-permute-start(f32[256,256]{1,0:T(8,128)S(1)} %get-tuple-element.1133), channel_id=1, source_target_pairs={{4,0},{8,4},{12,8},{16,12},{20,16},{24,20},{28,24},{5,1},{9,5},{13... | collective-permute-start | bytes 786440 | tf_op jit(solution)/shard_map/while/body/eval_jaxpr/ppermute | solution.py:17
  135.1 16.3 %collective-permute-start.2 = (f32[256,256]{1,0:T(8,128)S(1)}, f32[256,256]{1,0:T(8,128)S(1)}, u32[]{:S(2)}, u32[]{:S(2)}) collective-permute-start(f32[256,256]{1,0:T(8,128)S(1)} %get-tuple-element.1135), channel_id=1, source_target_pairs={{0,4},{4,8},{8,12},{12,16},{16,20},{20,24},{24,28},{1,5},{5,9},{9,... | collective-permute-start | bytes 786440 | tf_op jit(solution)/shard_map/while/body/eval_jaxpr/ppermute | solution.py:14
  153.2 23.5 %collective-permute-start.3 = (f32[256,256]{1,0:T(8,128)S(1)}, f32[256,256]{1,0:T(8,128)S(1)}, u32[]{:S(2)}, u32[]{:S(2)}) collective-permute-start(f32[256,256]{1,0:T(8,128)S(1)} %get-tuple-element.1137), channel_id=1, source_target_pairs={{4,0},{8,4},{12,8},{16,12},{20,16},{24,20},{28,24},{5,1},{9,5},{13... | collective-permute-start | bytes 786440 | tf_op jit(solution)/shard_map/while/body/eval_jaxpr/ppermute | solution.py:17
  176.7 17.5 %collective-permute-start = (f32[256,256]{1,0:T(8,128)S(1)}, f32[256,256]{1,0:T(8,128)S(1)}, u32[]{:S(2)}, u32[]{:S(2)}) collective-permute-start(f32[256,256]{1,0:T(8,128)S(1)} %get-tuple-element.1131), channel_id=1, source_target_pairs={{0,4},{4,8},{8,12},{12,16},{16,20},{20,24},{24,28},{1,5},{5,9},{9,... | collective-permute-start | bytes 786440 | tf_op jit(solution)/shard_map/while/body/eval_jaxpr/ppermute | solution.py:14
  196.0 23.5 %collective-permute-start.1 = (f32[256,256]{1,0:T(8,128)S(1)}, f32[256,256]{1,0:T(8,128)S(1)}, u32[]{:S(2)}, u32[]{:S(2)}) collective-permute-start(f32[256,256]{1,0:T(8,128)S(1)} %get-tuple-element.1133), channel_id=1, source_target_pairs={{4,0},{8,4},{12,8},{16,12},{20,16},{24,20},{28,24},{5,1},{9,5},{13... | collective-permute-start | bytes 786440 | tf_op jit(solution)/shard_map/while/body/eval_jaxpr/ppermute | solution.py:17
  219.5 18.4 %collective-permute-start.2 = (f32[256,256]{1,0:T(8,128)S(1)}, f32[256,256]{1,0:T(8,128)S(1)}, u32[]{:S(2)}, u32[]{:S(2)}) collective-permute-start(f32[256,256]{1,0:T(8,128)S(1)} %get-tuple-element.1135), channel_id=1, source_target_pairs={{0,4},{4,8},{8,12},{12,16},{16,20},{20,24},{24,28},{1,5},{5,9},{9,... | collective-permute-start | bytes 786440 | tf_op jit(solution)/shard_map/while/body/eval_jaxpr/ppermute | solution.py:14
  239.7 9.5 %collective-permute-start.3 = (f32[256,256]{1,0:T(8,128)S(1)}, f32[256,256]{1,0:T(8,128)S(1)}, u32[]{:S(2)}, u32[]{:S(2)}) collective-permute-start(f32[256,256]{1,0:T(8,128)S(1)} %get-tuple-element.1137), channel_id=1, source_target_pairs={{4,0},{8,4},{12,8},{16,12},{20,16},{24,20},{28,24},{5,1},{9,5},{13... | collective-permute-start | bytes 786440 | tf_op jit(solution)/shard_map/while/body/eval_jaxpr/ppermute | solution.py:17
  250.5 1.9 copy-start
  262.5 5.2 collective-permute-start
  269.5 9.3 %collective-permute-start.1 = (f32[256,256]{1,0:T(8,128)S(1)}, f32[256,256]{1,0:T(8,128)S(1)}, u32[]{:S(2)}, u32[]{:S(2)}) collective-permute-start(f32[256,256]{1,0:T(8,128)S(1)} %get-tuple-element.1133), channel_id=1, source_target_pairs={{4,0},{8,4},{12,8},{16,12},{20,16},{24,20},{28,24},{5,1},{9,5},{13... | collective-permute-start | bytes 786440 | tf_op jit(solution)/shard_map/while/body/eval_jaxpr/ppermute | solution.py:17
  280.1 1.9 copy-start.1
  292.1 5.2 collective-permute-start.2
  299.1 8.6 %collective-permute-start.3 = (f32[256,256]{1,0:T(8,128)S(1)}, f32[256,256]{1,0:T(8,128)S(1)}, u32[]{:S(2)}, u32[]{:S(2)}) collective-permute-start(f32[256,256]{1,0:T(8,128)S(1)} %get-tuple-element.1137), channel_id=1, source_target_pairs={{4,0},{8,4},{12,8},{16,12},{20,16},{24,20},{28,24},{5,1},{9,5},{13... | collective-permute-start | bytes 786440 | tf_op jit(solution)/shard_map/while/body/eval_jaxpr/ppermute | solution.py:17
  309.1 1.9 copy-start
  321.0 5.2 collective-permute-start
  328.1 9.8 %collective-permute-start.1 = (f32[256,256]{1,0:T(8,128)S(1)}, f32[256,256]{1,0:T(8,128)S(1)}, u32[]{:S(2)}, u32[]{:S(2)}) collective-permute-start(f32[256,256]{1,0:T(8,128)S(1)} %get-tuple-element.1133), channel_id=1, source_target_pairs={{4,0},{8,4},{12,8},{16,12},{20,16},{24,20},{28,24},{5,1},{9,5},{13... | collective-permute-start | bytes 786440 | tf_op jit(solution)/shard_map/while/body/eval_jaxpr/ppermute | solution.py:17
  339.1 1.9 copy-start.1
  350.5 5.7 %collective-permute-start.2 = (f32[256,256]{1,0:T(8,128)S(1)}, f32[256,256]{1,0:T(8,128)S(1)}, u32[]{:S(2)}, u32[]{:S(2)}) collective-permute-start(f32[256,256]{1,0:T(8,128)S(1)} %get-tuple-element.1135), channel_id=1, source_target_pairs={{0,4},{4,8},{8,12},{12,16},{16,20},{20,24},{24,28},{1,5},{5,9},{9,... | collective-permute-start | bytes 786440 | tf_op jit(solution)/shard_map/while/body/eval_jaxpr/ppermute | solution.py:14
  358.0 9.5 %collective-permute-start.3 = (f32[256,256]{1,0:T(8,128)S(1)}, f32[256,256]{1,0:T(8,128)S(1)}, u32[]{:S(2)}, u32[]{:S(2)}) collective-permute-start(f32[256,256]{1,0:T(8,128)S(1)} %get-tuple-element.1137), channel_id=1, source_target_pairs={{4,0},{8,4},{12,8},{16,12},{20,16},{24,20},{28,24},{5,1},{9,5},{13... | collective-permute-start | bytes 786440 | tf_op jit(solution)/shard_map/while/body/eval_jaxpr/ppermute | solution.py:17
  368.9 1.9 copy-start
  380.9 5.2 collective-permute-start
  387.9 9.3 %collective-permute-start.1 = (f32[256,256]{1,0:T(8,128)S(1)}, f32[256,256]{1,0:T(8,128)S(1)}, u32[]{:S(2)}, u32[]{:S(2)}) collective-permute-start(f32[256,256]{1,0:T(8,128)S(1)} %get-tuple-element.1133), channel_id=1, source_target_pairs={{4,0},{8,4},{12,8},{16,12},{20,16},{24,20},{28,24},{5,1},{9,5},{13... | collective-permute-start | bytes 786440 | tf_op jit(solution)/shard_map/while/body/eval_jaxpr/ppermute | solution.py:17
  398.5 1.9 copy-start.1
  410.5 5.2 collective-permute-start.2
  417.5 8.6 %collective-permute-start.3 = (f32[256,256]{1,0:T(8,128)S(1)}, f32[256,256]{1,0:T(8,128)S(1)}, u32[]{:S(2)}, u32[]{:S(2)}) collective-permute-start(f32[256,256]{1,0:T(8,128)S(1)} %get-tuple-element.1137), channel_id=1, source_target_pairs={{4,0},{8,4},{12,8},{16,12},{20,16},{24,20},{28,24},{5,1},{9,5},{13... | collective-permute-start | bytes 786440 | tf_op jit(solution)/shard_map/while/body/eval_jaxpr/ppermute | solution.py:17
  427.5 1.9 copy-start
  439.4 5.2 collective-permute-start
  446.4 8.4 %collective-permute-start.1 = (f32[256,256]{1,0:T(8,128)S(1)}, f32[256,256]{1,0:T(8,128)S(1)}, u32[]{:S(2)}, u32[]{:S(2)}) collective-permute-start(f32[256,256]{1,0:T(8,128)S(1)} %get-tuple-element.1133), channel_id=1, source_target_pairs={{4,0},{8,4},{12,8},{16,12},{20,16},{24,20},{28,24},{5,1},{9,5},{13... | collective-permute-start | bytes 786440 | tf_op jit(solution)/shard_map/while/body/eval_jaxpr/ppermute | solution.py:17
  456.1 1.9 copy-start.1
  467.5 5.2 collective-permute-start.2
  474.5 8.4 %collective-permute-start.3 = (f32[256,256]{1,0:T(8,128)S(1)}, f32[256,256]{1,0:T(8,128)S(1)}, u32[]{:S(2)}, u32[]{:S(2)}) collective-permute-start(f32[256,256]{1,0:T(8,128)S(1)} %get-tuple-element.1137), channel_id=1, source_target_pairs={{4,0},{8,4},{12,8},{16,12},{20,16},{24,20},{28,24},{5,1},{9,5},{13... | collective-permute-start | bytes 786440 | tf_op jit(solution)/shard_map/while/body/eval_jaxpr/ppermute | solution.py:17
  482.9 9.9 %collective-permute-start = (f32[256,256]{1,0:T(8,128)S(1)}, f32[256,256]{1,0:T(8,128)S(1)}, u32[]{:S(2)}, u32[]{:S(2)}) collective-permute-start(f32[256,256]{1,0:T(8,128)S(1)} %get-tuple-element.1131), channel_id=1, source_target_pairs={{0,4},{4,8},{8,12},{12,16},{16,20},{20,24},{24,28},{1,5},{5,9},{9,... | collective-permute-start | bytes 786440 | tf_op jit(solution)/shard_map/while/body/eval_jaxpr/ppermute | solution.py:14
  494.6 10.3 %collective-permute-start.1 = (f32[256,256]{1,0:T(8,128)S(1)}, f32[256,256]{1,0:T(8,128)S(1)}, u32[]{:S(2)}, u32[]{:S(2)}) collective-permute-start(f32[256,256]{1,0:T(8,128)S(1)} %get-tuple-element.1133), channel_id=1, source_target_pairs={{4,0},{8,4},{12,8},{16,12},{20,16},{24,20},{28,24},{5,1},{9,5},{13... | collective-permute-start | bytes 786440 | tf_op jit(solution)/shard_map/while/body/eval_jaxpr/ppermute | solution.py:17
  504.9 5.2 collective-permute-start.2
  511.9 8.4 %collective-permute-start.3 = (f32[256,256]{1,0:T(8,128)S(1)}, f32[256,256]{1,0:T(8,128)S(1)}, u32[]{:S(2)}, u32[]{:S(2)}) collective-permute-start(f32[256,256]{1,0:T(8,128)S(1)} %get-tuple-element.1137), channel_id=1, source_target_pairs={{4,0},{8,4},{12,8},{16,12},{20,16},{24,20},{28,24},{5,1},{9,5},{13... | collective-permute-start | bytes 786440 | tf_op jit(solution)/shard_map/while/body/eval_jaxpr/ppermute | solution.py:17
Sparse Core Ops, SparseCore 0:
  9.9 29.5 all-gather.4
  41.0 45.3 all-gather.2
where the time goes:
time: 530 us; the launch traced here: 527 us
  waiting for transfers between devices  276 us (52%)
  starting transfers between devices  100 us (19%)
  local copies, waits for them, and re-layouts  55.8 us (11%)
  matrix products  32.2 us (6%)
  other arithmetic  29 us (5%)
  loops' own time  20.7 us (4%)
  between operations  13.4 us (3%)
    ppermute x16, waiting for transfers between devices, extended_2(): lax.ppermute(lax.slice_in_dim(block, 0, width, axis=dim), axis, backward)  142 us
    ppermute x16, starting transfers between devices, extended_2(): lax.ppermute(lax.slice_in_dim(block, block.shape[dim] - width, None, axis...  69.6 us
    ppermute x16, waiting for transfers between devices, extended_2(): lax.ppermute(lax.slice_in_dim(block, block.shape[dim] - width, None, axis...  57.1 us
    all_gather x1, waiting for transfers between devices, per_device(): lax.all_gather(reflector_vectors, 'col', axis=2, tiled=True)  46.9 us
    ppermute x16, starting transfers between devices, extended_2(): lax.ppermute(lax.slice_in_dim(block, 0, width, axis=dim), axis, backward)  30.7 us
    all_gather x1, waiting for transfers between devices, per_device(): lax.all_gather(reflector_factors, 'col', axis=2, tiled=True)  29 us
    dynamic_slice x16, other arithmetic, one_step(): lax.dynamic_slice(field_now, (0, col_start), (reflect, piece_cols))  28.5 us
    dynamic_update_slice x8, local copies, waits for them, and re-layouts, work(): lax.dynamic_update_slice_in_dim(field_in, extended[:row_dev], col_start, 1)  26.5 us
  transfers between devices with their start and end apart: 34, of which 34 were waited for; matrix products, arithmetic and copies ran while one was open for 0% of the time, Pallas kernels for 0%

commit v1 on v0

--- a/solution.py
+++ b/solution.py
@@ -4,6 +4,12 @@
 from jax.sharding import PartitionSpec as P
 
 exact_mode = lax.Precision.HIGHEST
+
+
+def tiled_gather(x, axis, dim):
+    count = lax.axis_size(axis)
+    repeats = [count if d == dim else 1 for d in range(x.ndim)]
+    return lax.all_to_all(jnp.tile(x, repeats), axis, split_axis=dim, concat_axis=dim, tiled=True)
 
 
 def extended_2(block, sides, width):
@@ -44,7 +50,7 @@
     sweep_count = reflector_vectors.shape[0]
     vectors_all, factors_all = (
         lax.all_gather(reflector_vectors, "col", axis=2, tiled=True),
-        lax.all_gather(reflector_factors, "col", axis=2, tiled=True),
+        tiled_gather(reflector_factors, "col", 2),
     )
     pieces = 4
     piece_cols = col_count // pieces

time: 530 us -> 524 us (0.989)
  waiting for transfers between devices: 276 us -> 260 us
  starting transfers between devices: 100 us -> 106 us
    all_to_all x0 -> x1, waiting for transfers between devices: none -> 47.4 us  [tiled_gather(): lax.all_to_all(jnp.tile(x, repeats), axis, split_axis=dim, concat_axis=di...]
    all_gather x1, waiting for transfers between devices: 46.9 us -> 12.8 us  [per_device(): lax.all_gather(reflector_vectors, 'col', axis=2, tiled=True)]
    all_gather x1 -> x0, waiting for transfers between devices: 29 us -> none  [per_device(): lax.all_gather(reflector_factors, 'col', axis=2, tiled=True)]
    all_to_all x0 -> x1, starting transfers between devices: none -> 5.54 us  [tiled_gather(): lax.all_to_all(jnp.tile(x, repeats), axis, split_axis=dim, concat_axis=di...]
where the time goes in v1:
time: 524 us; the launch traced here: 521 us
  waiting for transfers between devices  260 us (50%)
  starting transfers between devices  106 us (20%)
  local copies, waits for them, and re-layouts  58.2 us (11%)
  matrix products  32.2 us (6%)
  other arithmetic  29 us (6%)
  loops' own time  21.8 us (4%)
  between operations  13.4 us (3%)
    ppermute x16, waiting for transfers between devices, extended_2(): lax.ppermute(lax.slice_in_dim(block, 0, width, axis=dim), axis, backward)  143 us
    ppermute x16, starting transfers between devices, extended_2(): lax.ppermute(lax.slice_in_dim(block, block.shape[dim] - width, None, axis...  70 us
    ppermute x16, waiting for transfers between devices, extended_2(): lax.ppermute(lax.slice_in_dim(block, block.shape[dim] - width, None, axis...  57.4 us
    all_to_all x1, waiting for transfers between devices, tiled_gather(): lax.all_to_all(jnp.tile(x, repeats), axis, split_axis=dim, concat_axis=di...  47.4 us
    ppermute x16, starting transfers between devices, extended_2(): lax.ppermute(lax.slice_in_dim(block, 0, width, axis=dim), axis, backward)  30.7 us
    dynamic_slice x16, other arithmetic, one_step(): lax.dynamic_slice(field_now, (0, col_start), (reflect, piece_cols))  28.5 us
    dynamic_update_slice x8, local copies, waits for them, and re-layouts, work(): lax.dynamic_update_slice_in_dim(field_in, extended[:row_dev], col_start, 1)  26.5 us
    another operation x8, loops' own time, work(): extended = lax.fori_loop(0, blocks_dev, one_block, extended)  19.6 us
  transfers between devices with their start and end apart: 34, of which 34 were waited for; matrix products, arithmetic and copies ran while one was open for 0% of the time, Pallas kernels for 0%

profile of v1, /device:TPU:1, one launch (start us, length us, event | category | flops | bytes accessed | tf_op | source)
XLA Modules:
  0.0 521.3 jit_solution(10274150501410048753)
XLA Ops:
  6.5 3.2 copy.47
  11.3 5.5 %all-to-all-start = ((f32[2,2,256,256]{3,1,0,2:T(2,128)}), f32[2,2,256,256]{3,1,0,2:T(2,128)S(1)}, u32[]{:S(2)}, u32[]{:S(2)}) async-start(f32[2,2,256,256]{3,1,0,2:T(2,128)} %bitcast.12), calls=%async_computation | async-start | bytes 2097152 | tf_op jit(solution)/shard_map/all_to_all | solution.py:12
  16.8 47.4 %all-to-all-done = f32[2,2,256,256]{3,1,0,2:T(2,128)S(1)} async-done(((f32[2,2,256,256]{3,1,0,2:T(2,128)}), f32[2,2,256,256]{3,1,0,2:T(2,128)S(1)}, u32[]{:S(2)}, u32[]{:S(2)}) %all-to-all-start) | async-done | bytes 1048608 | tf_op jit(solution)/shard_map/all_to_all | solution.py:12
  64.4 12.8 %all-gather.2.cloned.1.call-done = f32[2,2,256,512]{3,2,1,0:T(8,128)} async-done(((f32[2,2,64,512]{3,2,1,0:T(8,128)}), f32[2,2,256,512]{3,2,1,0:T(8,128)}) %all-gather.2.cloned.1.call-update) | async-done | bytes 2097168 | tf_op jit(solution)/shard_map/all_gather | solution.py:52
  77.2 437.3 %while.66 = (s32[]{:T(128)}, f32[512,1024]{1,0:T(8,128)}, f32[256,256]{1,0:T(8,128)S(1)}, s32[]{:T(128)}, s32[2,2]{1,0:T(2,128)S(1)}, /*index=5*/f32[2,2,256,512...) while((s32[]{:T(128)}, f32[512,1024]{1,0:T(8,128)}, ...), condition=%wide.region_13.14_spmd, body=%wide.region_0.13_spmd.sunk | while | flops 2014052352 | bytes 31459644 | solution.py:116
  77.3 3.5 collective-permute-start
  80.8 3.3 collective-permute-done
  87.8 6.5 %collective-permute-done.1 = f32[256,256]{1,0:T(8,128)S(1)} collective-permute-done((f32[256,256]{1,0:T(8,128)S(1)}, f32[256,256]{1,0:T(8,128)S(1)}, u32[]{:S(2)}, u32[]{:S(2)}) %collective-permute-start.1) | collective-permute-done | bytes 262176 | tf_op jit(solution)/shard_map/while/body/eval_jaxpr/ppermute | solution.py:23
  96.2 3.3 collective-permute-done.2
  103.2 6.5 %collective-permute-done.3 = f32[256,256]{1,0:T(8,128)S(1)} collective-permute-done((f32[256,256]{1,0:T(8,128)S(1)}, f32[256,256]{1,0:T(8,128)S(1)}, u32[]{:S(2)}, u32[]{:S(2)}) %collective-permute-start.3) | collective-permute-done | bytes 262176 | tf_op jit(solution)/shard_map/while/body/eval_jaxpr/ppermute | solution.py:23
  111.6 3.3 collective-permute-done
  118.6 7.6 %collective-permute-done.1 = f32[256,256]{1,0:T(8,128)S(1)} collective-permute-done((f32[256,256]{1,0:T(8,128)S(1)}, f32[256,256]{1,0:T(8,128)S(1)}, u32[]{:S(2)}, u32[]{:S(2)}) %collective-permute-start.1) | collective-permute-done | bytes 262176 | tf_op jit(solution)/shard_map/while/body/eval_jaxpr/ppermute | solution.py:23
  126.2 13.3 %collective-permute-start.2 = (f32[256,256]{1,0:T(8,128)S(1)}, f32[256,256]{1,0:T(8,128)S(1)}, u32[]{:S(2)}, u32[]{:S(2)}) collective-permute-start(f32[256,256]{1,0:T(8,128)S(1)} %get-tuple-element.1144), channel_id=1, source_target_pairs={{0,4},{4,8},{8,12},{12,16},{16,20},{20,24},{24,28},{1,5},{5,9},{9,... | collective-permute-start | bytes 786440 | tf_op jit(solution)/shard_map/while/body/eval_jaxpr/ppermute | solution.py:20
  139.5 3.3 collective-permute-done.2
  146.5 21.8 %collective-permute-done.3 = f32[256,256]{1,0:T(8,128)S(1)} collective-permute-done((f32[256,256]{1,0:T(8,128)S(1)}, f32[256,256]{1,0:T(8,128)S(1)}, u32[]{:S(2)}, u32[]{:S(2)}) %collective-permute-start.3) | collective-permute-done | bytes 262176 | tf_op jit(solution)/shard_map/while/body/eval_jaxpr/ppermute | solution.py:23
  168.3 14.4 %collective-permute-start = (f32[256,256]{1,0:T(8,128)S(1)}, f32[256,256]{1,0:T(8,128)S(1)}, u32[]{:S(2)}, u32[]{:S(2)}) collective-permute-start(f32[256,256]{1,0:T(8,128)S(1)} %get-tuple-element.1140), channel_id=1, source_target_pairs={{0,4},{4,8},{8,12},{12,16},{16,20},{20,24},{24,28},{1,5},{5,9},{9,... | collective-permute-start | bytes 786440 | tf_op jit(solution)/shard_map/while/body/eval_jaxpr/ppermute | solution.py:20
  182.7 3.3 collective-permute-done
  189.7 21.8 %collective-permute-done.1 = f32[256,256]{1,0:T(8,128)S(1)} collective-permute-done((f32[256,256]{1,0:T(8,128)S(1)}, f32[256,256]{1,0:T(8,128)S(1)}, u32[]{:S(2)}, u32[]{:S(2)}) %collective-permute-start.1) | collective-permute-done | bytes 262176 | tf_op jit(solution)/shard_map/while/body/eval_jaxpr/ppermute | solution.py:23
  211.5 15.3 %collective-permute-start.2 = (f32[256,256]{1,0:T(8,128)S(1)}, f32[256,256]{1,0:T(8,128)S(1)}, u32[]{:S(2)}, u32[]{:S(2)}) collective-permute-start(f32[256,256]{1,0:T(8,128)S(1)} %get-tuple-element.1144), channel_id=1, source_target_pairs={{0,4},{4,8},{8,12},{12,16},{16,20},{20,24},{24,28},{1,5},{5,9},{9,... | collective-permute-start | bytes 786440 | tf_op jit(solution)/shard_map/while/body/eval_jaxpr/ppermute | solution.py:20
  226.8 3.3 collective-permute-done.2
  233.8 7.6 %collective-permute-done.3 = f32[256,256]{1,0:T(8,128)S(1)} collective-permute-done((f32[256,256]{1,0:T(8,128)S(1)}, f32[256,256]{1,0:T(8,128)S(1)}, u32[]{:S(2)}, u32[]{:S(2)}) %collective-permute-start.3) | collective-permute-done | bytes 262176 | tf_op jit(solution)/shard_map/while/body/eval_jaxpr/ppermute | solution.py:23
  241.4 13.5 %conditional.8 = ((f32[512,1024]{1,0:T(8,128)}, f32[256,256]{1,0:T(8,128)S(1)})) conditional(s32[]{:T(128)} %convert_element_type.45, (f32[512,1024]{1,0:T(8,128)}, f32[256,256]{1,0:T(8,128)S(1)}) %tuple.172, (s32[]{:T(128)}, f32[512,1024]{1,0:T(8,128)}, f32[256,256]{1,0:T(8,128)S(1)}, s32[]{:T(128)}, pred[]{:T(512)}, ...), branch_computations={%region_1.1_spmd, %region_2.6_spmd} | conditional | flops 1006960640 | bytes 12321348 | solution.py:96
  244.8 6.6 %while.64 = (s32[]{:T(128)}, f32[768,256]{1,0:T(8,128)S(1)}, s32[]{:T(128)}, s32[]{:T(128)}, s32[]{:T(128)}, /*index=5*/f32[2,256,512]{2,1,0:T(8,128)S(1)}, f32[2,256,256]{2,1,0:T(8,128)S(1)}, s32[]{:T(128)}, s32[]{:T(128)}) while((s32[]{:T(128)}, f32[768,256]{1,0:T(8,128)S(1)}, s32[]{:T(128)}, s32[]{:T(128)}, s32[]{:T(128)}, ...), condition=%wide.region_6.5_spmd, body=%wide.region_3.4_spmd.sunk | while | flops 1006764032 | bytes 3932463 | solution.py:92
  251.5 3.5 dynamic_update_slice.35
  256.9 3.3 collective-permute-done
  263.9 7.4 %collective-permute-done.1 = f32[256,256]{1,0:T(8,128)S(1)} collective-permute-done((f32[256,256]{1,0:T(8,128)S(1)}, f32[256,256]{1,0:T(8,128)S(1)}, u32[]{:S(2)}, u32[]{:S(2)}) %collective-permute-start.1) | collective-permute-done | bytes 262176 | tf_op jit(solution)/shard_map/while/body/eval_jaxpr/ppermute | solution.py:23
  271.3 13.5 %conditional.9 = ((f32[512,1024]{1,0:T(8,128)}, f32[256,256]{1,0:T(8,128)S(1)})) conditional(s32[]{:T(128)} %convert_element_type.44, (f32[512,1024]{1,0:T(8,128)}, f32[256,256]{1,0:T(8,128)S(1)}) %tuple.174, (s32[]{:T(128)}, f32[512,1024]{1,0:T(8,128)}, f32[256,256]{1,0:T(8,128)S(1)}, s32[]{:T(128)}, pred[]{:T(512)}, ...), branch_computations={%region_7.7_spmd, %region_8.12_spmd} | conditional | flops 1006960640 | bytes 12321348 | solution.py:96
  274.7 6.6 %while.65 = (s32[]{:T(128)}, f32[768,256]{1,0:T(8,128)S(1)}, s32[]{:T(128)}, s32[]{:T(128)}, s32[]{:T(128)}, /*index=5*/f32[2,256,512]{2,1,0:T(8,128)S(1)}, f32[2,256,256]{2,1,0:T(8,128)S(1)}, s32[]{:T(128)}, s32[]{:T(128)}) while((s32[]{:T(128)}, f32[768,256]{1,0:T(8,128)S(1)}, s32[]{:T(128)}, s32[]{:T(128)}, s32[]{:T(128)}, ...), condition=%wide.region_12.11_spmd, body=%wide.region_9.10_spmd.sunk | while | flops 1006764032 | bytes 3932463 | solution.py:92
  281.3 3.5 dynamic_update_slice.37
  286.8 3.3 collective-permute-done.2
  293.7 6.7 %collective-permute-done.3 = f32[256,256]{1,0:T(8,128)S(1)} collective-permute-done((f32[256,256]{1,0:T(8,128)S(1)}, f32[256,256]{1,0:T(8,128)S(1)}, u32[]{:S(2)}, u32[]{:S(2)}) %collective-permute-start.3) | collective-permute-done | bytes 262176 | tf_op jit(solution)/shard_map/while/body/eval_jaxpr/ppermute | solution.py:23
  300.5 13.5 %conditional.8 = ((f32[512,1024]{1,0:T(8,128)}, f32[256,256]{1,0:T(8,128)S(1)})) conditional(s32[]{:T(128)} %convert_element_type.45, (f32[512,1024]{1,0:T(8,128)}, f32[256,256]{1,0:T(8,128)S(1)}) %tuple.172, (s32[]{:T(128)}, f32[512,1024]{1,0:T(8,128)}, f32[256,256]{1,0:T(8,128)S(1)}, s32[]{:T(128)}, pred[]{:T(512)}, ...), branch_computations={%region_1.1_spmd, %region_2.6_spmd} | conditional | flops 1006960640 | bytes 12321348 | solution.py:96
  303.9 6.6 %while.64 = (s32[]{:T(128)}, f32[768,256]{1,0:T(8,128)S(1)}, s32[]{:T(128)}, s32[]{:T(128)}, s32[]{:T(128)}, /*index=5*/f32[2,256,512]{2,1,0:T(8,128)S(1)}, f32[2,256,256]{2,1,0:T(8,128)S(1)}, s32[]{:T(128)}, s32[]{:T(128)}) while((s32[]{:T(128)}, f32[768,256]{1,0:T(8,128)S(1)}, s32[]{:T(128)}, s32[]{:T(128)}, s32[]{:T(128)}, ...), condition=%wide.region_6.5_spmd, body=%wide.region_3.4_spmd.sunk | while | flops 1006764032 | bytes 3932463 | solution.py:92
  310.5 3.5 dynamic_update_slice.35
  316.0 3.3 collective-permute-done
  323.0 7.9 %collective-permute-done.1 = f32[256,256]{1,0:T(8,128)S(1)} collective-permute-done((f32[256,256]{1,0:T(8,128)S(1)}, f32[256,256]{1,0:T(8,128)S(1)}, u32[]{:S(2)}, u32[]{:S(2)}) %collective-permute-start.1) | collective-permute-done | bytes 262176 | tf_op jit(solution)/shard_map/while/body/eval_jaxpr/ppermute | solution.py:23
  330.9 12.8 %conditional.9 = ((f32[512,1024]{1,0:T(8,128)}, f32[256,256]{1,0:T(8,128)S(1)})) conditional(s32[]{:T(128)} %convert_element_type.44, (f32[512,1024]{1,0:T(8,128)}, f32[256,256]{1,0:T(8,128)S(1)}) %tuple.174, (s32[]{:T(128)}, f32[512,1024]{1,0:T(8,128)}, f32[256,256]{1,0:T(8,128)S(1)}, s32[]{:T(128)}, pred[]{:T(512)}, ...), branch_computations={%region_7.7_spmd, %region_8.12_spmd} | conditional | flops 1006960640 | bytes 12321348 | solution.py:96
  334.2 6.6 %while.65 = (s32[]{:T(128)}, f32[768,256]{1,0:T(8,128)S(1)}, s32[]{:T(128)}, s32[]{:T(128)}, s32[]{:T(128)}, /*index=5*/f32[2,256,512]{2,1,0:T(8,128)S(1)}, f32[2,256,256]{2,1,0:T(8,128)S(1)}, s32[]{:T(128)}, s32[]{:T(128)}) while((s32[]{:T(128)}, f32[768,256]{1,0:T(8,128)S(1)}, s32[]{:T(128)}, s32[]{:T(128)}, s32[]{:T(128)}, ...), condition=%wide.region_12.11_spmd, body=%wide.region_9.10_spmd.sunk | while | flops 1006764032 | bytes 3932463 | solution.py:92
  340.8 2.9 dynamic_update_slice.37
  346.2 3.3 collective-permute-done.2
  353.2 7.6 %collective-permute-done.3 = f32[256,256]{1,0:T(8,128)S(1)} collective-permute-done((f32[256,256]{1,0:T(8,128)S(1)}, f32[256,256]{1,0:T(8,128)S(1)}, u32[]{:S(2)}, u32[]{:S(2)}) %collective-permute-start.3) | collective-permute-done | bytes 262176 | tf_op jit(solution)/shard_map/while/body/eval_jaxpr/ppermute | solution.py:23
  360.7 13.5 %conditional.8 = ((f32[512,1024]{1,0:T(8,128)}, f32[256,256]{1,0:T(8,128)S(1)})) conditional(s32[]{:T(128)} %convert_element_type.45, (f32[512,1024]{1,0:T(8,128)}, f32[256,256]{1,0:T(8,128)S(1)}) %tuple.172, (s32[]{:T(128)}, f32[512,1024]{1,0:T(8,128)}, f32[256,256]{1,0:T(8,128)S(1)}, s32[]{:T(128)}, pred[]{:T(512)}, ...), branch_computations={%region_1.1_spmd, %region_2.6_spmd} | conditional | flops 1006960640 | bytes 12321348 | solution.py:96
  364.2 6.6 %while.64 = (s32[]{:T(128)}, f32[768,256]{1,0:T(8,128)S(1)}, s32[]{:T(128)}, s32[]{:T(128)}, s32[]{:T(128)}, /*index=5*/f32[2,256,512]{2,1,0:T(8,128)S(1)}, f32[2,256,256]{2,1,0:T(8,128)S(1)}, s32[]{:T(128)}, s32[]{:T(128)}) while((s32[]{:T(128)}, f32[768,256]{1,0:T(8,128)S(1)}, s32[]{:T(128)}, s32[]{:T(128)}, s32[]{:T(128)}, ...), condition=%wide.region_6.5_spmd, body=%wide.region_3.4_spmd.sunk | while | flops 1006764032 | bytes 3932463 | solution.py:92
  370.8 3.5 dynamic_update_slice.35
  376.2 3.3 collective-permute-done
  383.2 7.4 %collective-permute-done.1 = f32[256,256]{1,0:T(8,128)S(1)} collective-permute-done((f32[256,256]{1,0:T(8,128)S(1)}, f32[256,256]{1,0:T(8,128)S(1)}, u32[]{:S(2)}, u32[]{:S(2)}) %collective-permute-start.1) | collective-permute-done | bytes 262176 | tf_op jit(solution)/shard_map/while/body/eval_jaxpr/ppermute | solution.py:23
  390.6 13.5 %conditional.9 = ((f32[512,1024]{1,0:T(8,128)}, f32[256,256]{1,0:T(8,128)S(1)})) conditional(s32[]{:T(128)} %convert_element_type.44, (f32[512,1024]{1,0:T(8,128)}, f32[256,256]{1,0:T(8,128)S(1)}) %tuple.174, (s32[]{:T(128)}, f32[512,1024]{1,0:T(8,128)}, f32[256,256]{1,0:T(8,128)S(1)}, s32[]{:T(128)}, pred[]{:T(512)}, ...), branch_computations={%region_7.7_spmd, %region_8.12_spmd} | conditional | flops 1006960640 | bytes 12321348 | solution.py:96
  394.0 6.6 %while.65 = (s32[]{:T(128)}, f32[768,256]{1,0:T(8,128)S(1)}, s32[]{:T(128)}, s32[]{:T(128)}, s32[]{:T(128)}, /*index=5*/f32[2,256,512]{2,1,0:T(8,128)S(1)}, f32[2,256,256]{2,1,0:T(8,128)S(1)}, s32[]{:T(128)}, s32[]{:T(128)}) while((s32[]{:T(128)}, f32[768,256]{1,0:T(8,128)S(1)}, s32[]{:T(128)}, s32[]{:T(128)}, s32[]{:T(128)}, ...), condition=%wide.region_12.11_spmd, body=%wide.region_9.10_spmd.sunk | while | flops 1006764032 | bytes 3932463 | solution.py:92
  400.7 3.5 dynamic_update_slice.37
  406.1 3.3 collective-permute-done.2
  413.1 6.7 %collective-permute-done.3 = f32[256,256]{1,0:T(8,128)S(1)} collective-permute-done((f32[256,256]{1,0:T(8,128)S(1)}, f32[256,256]{1,0:T(8,128)S(1)}, u32[]{:S(2)}, u32[]{:S(2)}) %collective-permute-start.3) | collective-permute-done | bytes 262176 | tf_op jit(solution)/shard_map/while/body/eval_jaxpr/ppermute | solution.py:23
  419.8 13.5 %conditional.8 = ((f32[512,1024]{1,0:T(8,128)}, f32[256,256]{1,0:T(8,128)S(1)})) conditional(s32[]{:T(128)} %convert_element_type.45, (f32[512,1024]{1,0:T(8,128)}, f32[256,256]{1,0:T(8,128)S(1)}) %tuple.172, (s32[]{:T(128)}, f32[512,1024]{1,0:T(8,128)}, f32[256,256]{1,0:T(8,128)S(1)}, s32[]{:T(128)}, pred[]{:T(512)}, ...), branch_computations={%region_1.1_spmd, %region_2.6_spmd} | conditional | flops 1006960640 | bytes 12321348 | solution.py:96
  423.2 6.6 %while.64 = (s32[]{:T(128)}, f32[768,256]{1,0:T(8,128)S(1)}, s32[]{:T(128)}, s32[]{:T(128)}, s32[]{:T(128)}, /*index=5*/f32[2,256,512]{2,1,0:T(8,128)S(1)}, f32[2,256,256]{2,1,0:T(8,128)S(1)}, s32[]{:T(128)}, s32[]{:T(128)}) while((s32[]{:T(128)}, f32[768,256]{1,0:T(8,128)S(1)}, s32[]{:T(128)}, s32[]{:T(128)}, s32[]{:T(128)}, ...), condition=%wide.region_6.5_spmd, body=%wide.region_3.4_spmd.sunk | while | flops 1006764032 | bytes 3932463 | solution.py:92
  429.8 3.5 dynamic_update_slice.35
  435.3 3.3 collective-permute-done
  442.3 6.5 %collective-permute-done.1 = f32[256,256]{1,0:T(8,128)S(1)} collective-permute-done((f32[256,256]{1,0:T(8,128)S(1)}, f32[256,256]{1,0:T(8,128)S(1)}, u32[]{:S(2)}, u32[]{:S(2)}) %collective-permute-start.1) | collective-permute-done | bytes 262176 | tf_op jit(solution)/shard_map/while/body/eval_jaxpr/ppermute | solution.py:23
  448.8 12.8 %conditional.9 = ((f32[512,1024]{1,0:T(8,128)}, f32[256,256]{1,0:T(8,128)S(1)})) conditional(s32[]{:T(128)} %convert_element_type.44, (f32[512,1024]{1,0:T(8,128)}, f32[256,256]{1,0:T(8,128)S(1)}) %tuple.174, (s32[]{:T(128)}, f32[512,1024]{1,0:T(8,128)}, f32[256,256]{1,0:T(8,128)S(1)}, s32[]{:T(128)}, pred[]{:T(512)}, ...), branch_computations={%region_7.7_spmd, %region_8.12_spmd} | conditional | flops 1006960640 | bytes 12321348 | solution.py:96
  452.1 6.6 %while.65 = (s32[]{:T(128)}, f32[768,256]{1,0:T(8,128)S(1)}, s32[]{:T(128)}, s32[]{:T(128)}, s32[]{:T(128)}, /*index=5*/f32[2,256,512]{2,1,0:T(8,128)S(1)}, f32[2,256,256]{2,1,0:T(8,128)S(1)}, s32[]{:T(128)}, s32[]{:T(128)}) while((s32[]{:T(128)}, f32[768,256]{1,0:T(8,128)S(1)}, s32[]{:T(128)}, s32[]{:T(128)}, s32[]{:T(128)}, ...), condition=%wide.region_12.11_spmd, body=%wide.region_9.10_spmd.sunk | while | flops 1006764032 | bytes 3932463 | solution.py:92
  463.6 3.3 collective-permute-done.2
  470.5 6.5 %collective-permute-done.3 = f32[256,256]{1,0:T(8,128)S(1)} collective-permute-done((f32[256,256]{1,0:T(8,128)S(1)}, f32[256,256]{1,0:T(8,128)S(1)}, u32[]{:S(2)}, u32[]{:S(2)}) %collective-permute-start.3) | collective-permute-done | bytes 262176 | tf_op jit(solution)/shard_map/while/body/eval_jaxpr/ppermute | solution.py:23
  479.0 8.2 %collective-permute-done = f32[256,256]{1,0:T(8,128)S(1)} collective-permute-done((f32[256,256]{1,0:T(8,128)S(1)}, f32[256,256]{1,0:T(8,128)S(1)}, u32[]{:S(2)}, u32[]{:S(2)}) %collective-permute-start) | collective-permute-done | bytes 262176 | tf_op jit(solution)/shard_map/while/body/eval_jaxpr/ppermute | solution.py:20
  491.1 8.0 %collective-permute-done.1 = f32[256,256]{1,0:T(8,128)S(1)} collective-permute-done((f32[256,256]{1,0:T(8,128)S(1)}, f32[256,256]{1,0:T(8,128)S(1)}, u32[]{:S(2)}, u32[]{:S(2)}) %collective-permute-start.1) | collective-permute-done | bytes 262176 | tf_op jit(solution)/shard_map/while/body/eval_jaxpr/ppermute | solution.py:23
  501.0 3.3 collective-permute-done.2
  508.0 6.5 %collective-permute-done.3 = f32[256,256]{1,0:T(8,128)S(1)} collective-permute-done((f32[256,256]{1,0:T(8,128)S(1)}, f32[256,256]{1,0:T(8,128)S(1)}, u32[]{:S(2)}, u32[]{:S(2)}) %collective-permute-start.3) | collective-permute-done | bytes 262176 | tf_op jit(solution)/shard_map/while/body/eval_jaxpr/ppermute | solution.py:23
  (183 shorter events, 179.8 us)
Async XLA Ops:
  6.5 3.2 copy-start
  6.5 70.6 %all-gather.2.cloned.1.call-start = ((), (), s32[]{:S(2)}) async-start(), calls=%async_computation.1 | async-start | bytes 2621440 | tf_op jit(solution)/shard_map/all_gather | solution.py:52
  11.3 65.9 %copy-start.1 = (s32[2,2]{1,0:T(2,128)S(1)}, s32[2,2]{1,0:T(2,128)}, u32[]{:S(2)}) copy-start(s32[2,2]{1,0:T(2,128)} %param.21) | copy-start | bytes 52
  11.3 52.9 %all-to-all-start = ((f32[2,2,256,256]{3,1,0,2:T(2,128)}), f32[2,2,256,256]{3,1,0,2:T(2,128)S(1)}, u32[]{:S(2)}, u32[]{:S(2)}) async-start(f32[2,2,256,256]{3,1,0,2:T(2,128)} %bitcast.12), calls=%async_computation | async-start | bytes 2097152 | tf_op jit(solution)/shard_map/all_to_all | solution.py:12
  77.3 6.8 %collective-permute-start = (f32[256,256]{1,0:T(8,128)S(1)}, f32[256,256]{1,0:T(8,128)S(1)}, u32[]{:S(2)}, u32[]{:S(2)}) collective-permute-start(f32[256,256]{1,0:T(8,128)S(1)} %get-tuple-element.1140), channel_id=1, source_target_pairs={{0,4},{4,8},{8,12},{12,16},{16,20},{20,24},{24,28},{1,5},{5,9},{9,... | collective-permute-start | bytes 786440 | tf_op jit(solution)/shard_map/while/body/eval_jaxpr/ppermute | solution.py:20
  85.8 8.4 %collective-permute-start.1 = (f32[256,256]{1,0:T(8,128)S(1)}, f32[256,256]{1,0:T(8,128)S(1)}, u32[]{:S(2)}, u32[]{:S(2)}) collective-permute-start(f32[256,256]{1,0:T(8,128)S(1)} %get-tuple-element.1142), channel_id=1, source_target_pairs={{4,0},{8,4},{12,8},{16,12},{20,16},{24,20},{28,24},{5,1},{9,5},{13... | collective-permute-start | bytes 786440 | tf_op jit(solution)/shard_map/while/body/eval_jaxpr/ppermute | solution.py:23
  94.3 5.2 collective-permute-start.2
  101.3 8.4 %collective-permute-start.3 = (f32[256,256]{1,0:T(8,128)S(1)}, f32[256,256]{1,0:T(8,128)S(1)}, u32[]{:S(2)}, u32[]{:S(2)}) collective-permute-start(f32[256,256]{1,0:T(8,128)S(1)} %get-tuple-element.1146), channel_id=1, source_target_pairs={{4,0},{8,4},{12,8},{16,12},{20,16},{24,20},{28,24},{5,1},{9,5},{13... | collective-permute-start | bytes 786440 | tf_op jit(solution)/shard_map/while/body/eval_jaxpr/ppermute | solution.py:23
  109.7 5.2 collective-permute-start
  116.7 9.5 %collective-permute-start.1 = (f32[256,256]{1,0:T(8,128)S(1)}, f32[256,256]{1,0:T(8,128)S(1)}, u32[]{:S(2)}, u32[]{:S(2)}) collective-permute-start(f32[256,256]{1,0:T(8,128)S(1)} %get-tuple-element.1142), channel_id=1, source_target_pairs={{4,0},{8,4},{12,8},{16,12},{20,16},{24,20},{28,24},{5,1},{9,5},{13... | collective-permute-start | bytes 786440 | tf_op jit(solution)/shard_map/while/body/eval_jaxpr/ppermute | solution.py:23
  126.2 16.6 %collective-permute-start.2 = (f32[256,256]{1,0:T(8,128)S(1)}, f32[256,256]{1,0:T(8,128)S(1)}, u32[]{:S(2)}, u32[]{:S(2)}) collective-permute-start(f32[256,256]{1,0:T(8,128)S(1)} %get-tuple-element.1144), channel_id=1, source_target_pairs={{0,4},{4,8},{8,12},{12,16},{16,20},{20,24},{24,28},{1,5},{5,9},{9,... | collective-permute-start | bytes 786440 | tf_op jit(solution)/shard_map/while/body/eval_jaxpr/ppermute | solution.py:20
  144.5 23.7 %collective-permute-start.3 = (f32[256,256]{1,0:T(8,128)S(1)}, f32[256,256]{1,0:T(8,128)S(1)}, u32[]{:S(2)}, u32[]{:S(2)}) collective-permute-start(f32[256,256]{1,0:T(8,128)S(1)} %get-tuple-element.1146), channel_id=1, source_target_pairs={{4,0},{8,4},{12,8},{16,12},{20,16},{24,20},{28,24},{5,1},{9,5},{13... | collective-permute-start | bytes 786440 | tf_op jit(solution)/shard_map/while/body/eval_jaxpr/ppermute | solution.py:23
  168.3 17.7 %collective-permute-start = (f32[256,256]{1,0:T(8,128)S(1)}, f32[256,256]{1,0:T(8,128)S(1)}, u32[]{:S(2)}, u32[]{:S(2)}) collective-permute-start(f32[256,256]{1,0:T(8,128)S(1)} %get-tuple-element.1140), channel_id=1, source_target_pairs={{0,4},{4,8},{8,12},{12,16},{16,20},{20,24},{24,28},{1,5},{5,9},{9,... | collective-permute-start | bytes 786440 | tf_op jit(solution)/shard_map/while/body/eval_jaxpr/ppermute | solution.py:20
  187.8 23.8 %collective-permute-start.1 = (f32[256,256]{1,0:T(8,128)S(1)}, f32[256,256]{1,0:T(8,128)S(1)}, u32[]{:S(2)}, u32[]{:S(2)}) collective-permute-start(f32[256,256]{1,0:T(8,128)S(1)} %get-tuple-element.1142), channel_id=1, source_target_pairs={{4,0},{8,4},{12,8},{16,12},{20,16},{24,20},{28,24},{5,1},{9,5},{13... | collective-permute-start | bytes 786440 | tf_op jit(solution)/shard_map/while/body/eval_jaxpr/ppermute | solution.py:23
  211.5 18.6 %collective-permute-start.2 = (f32[256,256]{1,0:T(8,128)S(1)}, f32[256,256]{1,0:T(8,128)S(1)}, u32[]{:S(2)}, u32[]{:S(2)}) collective-permute-start(f32[256,256]{1,0:T(8,128)S(1)} %get-tuple-element.1144), channel_id=1, source_target_pairs={{0,4},{4,8},{8,12},{12,16},{16,20},{20,24},{24,28},{1,5},{5,9},{9,... | collective-permute-start | bytes 786440 | tf_op jit(solution)/shard_map/while/body/eval_jaxpr/ppermute | solution.py:20
  231.9 9.5 %collective-permute-start.3 = (f32[256,256]{1,0:T(8,128)S(1)}, f32[256,256]{1,0:T(8,128)S(1)}, u32[]{:S(2)}, u32[]{:S(2)}) collective-permute-start(f32[256,256]{1,0:T(8,128)S(1)} %get-tuple-element.1146), channel_id=1, source_target_pairs={{4,0},{8,4},{12,8},{16,12},{20,16},{24,20},{28,24},{5,1},{9,5},{13... | collective-permute-start | bytes 786440 | tf_op jit(solution)/shard_map/while/body/eval_jaxpr/ppermute | solution.py:23
  254.9 5.2 %collective-permute-start = (f32[256,256]{1,0:T(8,128)S(1)}, f32[256,256]{1,0:T(8,128)S(1)}, u32[]{:S(2)}, u32[]{:S(2)}) collective-permute-start(f32[256,256]{1,0:T(8,128)S(1)} %get-tuple-element.1140), channel_id=1, source_target_pairs={{0,4},{4,8},{8,12},{12,16},{16,20},{20,24},{24,28},{1,5},{5,9},{9,... | collective-permute-start | bytes 786440 | tf_op jit(solution)/shard_map/while/body/eval_jaxpr/ppermute | solution.py:20
  262.0 9.3 %collective-permute-start.1 = (f32[256,256]{1,0:T(8,128)S(1)}, f32[256,256]{1,0:T(8,128)S(1)}, u32[]{:S(2)}, u32[]{:S(2)}) collective-permute-start(f32[256,256]{1,0:T(8,128)S(1)} %get-tuple-element.1142), channel_id=1, source_target_pairs={{4,0},{8,4},{12,8},{16,12},{20,16},{24,20},{28,24},{5,1},{9,5},{13... | collective-permute-start | bytes 786440 | tf_op jit(solution)/shard_map/while/body/eval_jaxpr/ppermute | solution.py:23
  284.8 5.2 %collective-permute-start.2 = (f32[256,256]{1,0:T(8,128)S(1)}, f32[256,256]{1,0:T(8,128)S(1)}, u32[]{:S(2)}, u32[]{:S(2)}) collective-permute-start(f32[256,256]{1,0:T(8,128)S(1)} %get-tuple-element.1144), channel_id=1, source_target_pairs={{0,4},{4,8},{8,12},{12,16},{16,20},{20,24},{24,28},{1,5},{5,9},{9,... | collective-permute-start | bytes 786440 | tf_op jit(solution)/shard_map/while/body/eval_jaxpr/ppermute | solution.py:20
  291.8 8.6 %collective-permute-start.3 = (f32[256,256]{1,0:T(8,128)S(1)}, f32[256,256]{1,0:T(8,128)S(1)}, u32[]{:S(2)}, u32[]{:S(2)}) collective-permute-start(f32[256,256]{1,0:T(8,128)S(1)} %get-tuple-element.1146), channel_id=1, source_target_pairs={{4,0},{8,4},{12,8},{16,12},{20,16},{24,20},{28,24},{5,1},{9,5},{13... | collective-permute-start | bytes 786440 | tf_op jit(solution)/shard_map/while/body/eval_jaxpr/ppermute | solution.py:23
  314.0 5.2 %collective-permute-start = (f32[256,256]{1,0:T(8,128)S(1)}, f32[256,256]{1,0:T(8,128)S(1)}, u32[]{:S(2)}, u32[]{:S(2)}) collective-permute-start(f32[256,256]{1,0:T(8,128)S(1)} %get-tuple-element.1140), channel_id=1, source_target_pairs={{0,4},{4,8},{8,12},{12,16},{16,20},{20,24},{24,28},{1,5},{5,9},{9,... | collective-permute-start | bytes 786440 | tf_op jit(solution)/shard_map/while/body/eval_jaxpr/ppermute | solution.py:20
  321.0 9.8 %collective-permute-start.1 = (f32[256,256]{1,0:T(8,128)S(1)}, f32[256,256]{1,0:T(8,128)S(1)}, u32[]{:S(2)}, u32[]{:S(2)}) collective-permute-start(f32[256,256]{1,0:T(8,128)S(1)} %get-tuple-element.1142), channel_id=1, source_target_pairs={{4,0},{8,4},{12,8},{16,12},{20,16},{24,20},{28,24},{5,1},{9,5},{13... | collective-permute-start | bytes 786440 | tf_op jit(solution)/shard_map/while/body/eval_jaxpr/ppermute | solution.py:23
  343.7 5.8 %collective-permute-start.2 = (f32[256,256]{1,0:T(8,128)S(1)}, f32[256,256]{1,0:T(8,128)S(1)}, u32[]{:S(2)}, u32[]{:S(2)}) collective-permute-start(f32[256,256]{1,0:T(8,128)S(1)} %get-tuple-element.1144), channel_id=1, source_target_pairs={{0,4},{4,8},{8,12},{12,16},{16,20},{20,24},{24,28},{1,5},{5,9},{9,... | collective-permute-start | bytes 786440 | tf_op jit(solution)/shard_map/while/body/eval_jaxpr/ppermute | solution.py:20
  351.2 9.5 %collective-permute-start.3 = (f32[256,256]{1,0:T(8,128)S(1)}, f32[256,256]{1,0:T(8,128)S(1)}, u32[]{:S(2)}, u32[]{:S(2)}) collective-permute-start(f32[256,256]{1,0:T(8,128)S(1)} %get-tuple-element.1146), channel_id=1, source_target_pairs={{4,0},{8,4},{12,8},{16,12},{20,16},{24,20},{28,24},{5,1},{9,5},{13... | collective-permute-start | bytes 786440 | tf_op jit(solution)/shard_map/while/body/eval_jaxpr/ppermute | solution.py:23
  374.3 5.2 %collective-permute-start = (f32[256,256]{1,0:T(8,128)S(1)}, f32[256,256]{1,0:T(8,128)S(1)}, u32[]{:S(2)}, u32[]{:S(2)}) collective-permute-start(f32[256,256]{1,0:T(8,128)S(1)} %get-tuple-element.1140), channel_id=1, source_target_pairs={{0,4},{4,8},{8,12},{12,16},{16,20},{20,24},{24,28},{1,5},{5,9},{9,... | collective-permute-start | bytes 786440 | tf_op jit(solution)/shard_map/while/body/eval_jaxpr/ppermute | solution.py:20
  381.3 9.3 %collective-permute-start.1 = (f32[256,256]{1,0:T(8,128)S(1)}, f32[256,256]{1,0:T(8,128)S(1)}, u32[]{:S(2)}, u32[]{:S(2)}) collective-permute-start(f32[256,256]{1,0:T(8,128)S(1)} %get-tuple-element.1142), channel_id=1, source_target_pairs={{4,0},{8,4},{12,8},{16,12},{20,16},{24,20},{28,24},{5,1},{9,5},{13... | collective-permute-start | bytes 786440 | tf_op jit(solution)/shard_map/while/body/eval_jaxpr/ppermute | solution.py:23
  404.2 5.2 %collective-permute-start.2 = (f32[256,256]{1,0:T(8,128)S(1)}, f32[256,256]{1,0:T(8,128)S(1)}, u32[]{:S(2)}, u32[]{:S(2)}) collective-permute-start(f32[256,256]{1,0:T(8,128)S(1)} %get-tuple-element.1144), channel_id=1, source_target_pairs={{0,4},{4,8},{8,12},{12,16},{16,20},{20,24},{24,28},{1,5},{5,9},{9,... | collective-permute-start | bytes 786440 | tf_op jit(solution)/shard_map/while/body/eval_jaxpr/ppermute | solution.py:20
  411.2 8.6 %collective-permute-start.3 = (f32[256,256]{1,0:T(8,128)S(1)}, f32[256,256]{1,0:T(8,128)S(1)}, u32[]{:S(2)}, u32[]{:S(2)}) collective-permute-start(f32[256,256]{1,0:T(8,128)S(1)} %get-tuple-element.1146), channel_id=1, source_target_pairs={{4,0},{8,4},{12,8},{16,12},{20,16},{24,20},{28,24},{5,1},{9,5},{13... | collective-permute-start | bytes 786440 | tf_op jit(solution)/shard_map/while/body/eval_jaxpr/ppermute | solution.py:23
  433.3 5.2 %collective-permute-start = (f32[256,256]{1,0:T(8,128)S(1)}, f32[256,256]{1,0:T(8,128)S(1)}, u32[]{:S(2)}, u32[]{:S(2)}) collective-permute-start(f32[256,256]{1,0:T(8,128)S(1)} %get-tuple-element.1140), channel_id=1, source_target_pairs={{0,4},{4,8},{8,12},{12,16},{16,20},{20,24},{24,28},{1,5},{5,9},{9,... | collective-permute-start | bytes 786440 | tf_op jit(solution)/shard_map/while/body/eval_jaxpr/ppermute | solution.py:20
  440.3 8.4 %collective-permute-start.1 = (f32[256,256]{1,0:T(8,128)S(1)}, f32[256,256]{1,0:T(8,128)S(1)}, u32[]{:S(2)}, u32[]{:S(2)}) collective-permute-start(f32[256,256]{1,0:T(8,128)S(1)} %get-tuple-element.1142), channel_id=1, source_target_pairs={{4,0},{8,4},{12,8},{16,12},{20,16},{24,20},{28,24},{5,1},{9,5},{13... | collective-permute-start | bytes 786440 | tf_op jit(solution)/shard_map/while/body/eval_jaxpr/ppermute | solution.py:23
  461.6 5.2 %collective-permute-start.2 = (f32[256,256]{1,0:T(8,128)S(1)}, f32[256,256]{1,0:T(8,128)S(1)}, u32[]{:S(2)}, u32[]{:S(2)}) collective-permute-start(f32[256,256]{1,0:T(8,128)S(1)} %get-tuple-element.1144), channel_id=1, source_target_pairs={{0,4},{4,8},{8,12},{12,16},{16,20},{20,24},{24,28},{1,5},{5,9},{9,... | collective-permute-start | bytes 786440 | tf_op jit(solution)/shard_map/while/body/eval_jaxpr/ppermute | solution.py:20
  468.6 8.4 %collective-permute-start.3 = (f32[256,256]{1,0:T(8,128)S(1)}, f32[256,256]{1,0:T(8,128)S(1)}, u32[]{:S(2)}, u32[]{:S(2)}) collective-permute-start(f32[256,256]{1,0:T(8,128)S(1)} %get-tuple-element.1146), channel_id=1, source_target_pairs={{4,0},{8,4},{12,8},{16,12},{20,16},{24,20},{28,24},{5,1},{9,5},{13... | collective-permute-start | bytes 786440 | tf_op jit(solution)/shard_map/while/body/eval_jaxpr/ppermute | solution.py:23
  477.1 10.2 %collective-permute-start = (f32[256,256]{1,0:T(8,128)S(1)}, f32[256,256]{1,0:T(8,128)S(1)}, u32[]{:S(2)}, u32[]{:S(2)}) collective-permute-start(f32[256,256]{1,0:T(8,128)S(1)} %get-tuple-element.1140), channel_id=1, source_target_pairs={{0,4},{4,8},{8,12},{12,16},{16,20},{20,24},{24,28},{1,5},{5,9},{9,... | collective-permute-start | bytes 786440 | tf_op jit(solution)/shard_map/while/body/eval_jaxpr/ppermute | solution.py:20
  489.0 10.1 %collective-permute-start.1 = (f32[256,256]{1,0:T(8,128)S(1)}, f32[256,256]{1,0:T(8,128)S(1)}, u32[]{:S(2)}, u32[]{:S(2)}) collective-permute-start(f32[256,256]{1,0:T(8,128)S(1)} %get-tuple-element.1142), channel_id=1, source_target_pairs={{4,0},{8,4},{12,8},{16,12},{20,16},{24,20},{28,24},{5,1},{9,5},{13... | collective-permute-start | bytes 786440 | tf_op jit(solution)/shard_map/while/body/eval_jaxpr/ppermute | solution.py:23
  499.0 5.2 collective-permute-start.2
  506.0 8.4 %collective-permute-start.3 = (f32[256,256]{1,0:T(8,128)S(1)}, f32[256,256]{1,0:T(8,128)S(1)}, u32[]{:S(2)}, u32[]{:S(2)}) collective-permute-start(f32[256,256]{1,0:T(8,128)S(1)} %get-tuple-element.1146), channel_id=1, source_target_pairs={{4,0},{8,4},{12,8},{16,12},{20,16},{24,20},{28,24},{5,1},{9,5},{13... | collective-permute-start | bytes 786440 | tf_op jit(solution)/shard_map/while/body/eval_jaxpr/ppermute | solution.py:23
Sparse Core Ops, SparseCore 0:
  9.9 67.2 all-gather.1
